TPU v7x, 32 devices: a whole 2x2x4 slice. The times are simulated.
32 devices in a mesh: rep: 8 (over y, x, core), shard: 4 (over z).
Axes of the slice: x: 2, y: 2, z: 4, core: 2. Of those that a mesh axis runs over, the one named last changes fastest.
Arguments:
- teacher_states: bfloat16 [3072, 5120], P('rep'), may hold values from -16 to 16
- student_states: bfloat16 [3072, 3584], P('rep'), may hold values from -16 to 16
- teacher_gain: float32 [5120], replicated, may hold values from 0.25 to 1.75
- student_gain: float32 [3584], replicated, may hold values from 0.25 to 1.75
- teacher_query: bfloat16 [5120, 3072], P('rep', 'shard'), may hold values from -1 to 1
- teacher_key: bfloat16 [5120, 1024], P('rep', 'shard'), may hold values from -1 to 1
- teacher_value: bfloat16 [5120, 1024], P('rep', 'shard'), may hold values from -0.078125 to 0.078125
- teacher_output: bfloat16 [5120, 3072], P('rep', 'shard'), may hold values from -0.109375 to 0.109375
- student_query: bfloat16 [3584, 2048], P('rep', 'shard'), may hold values from -1 to 1
- student_key: bfloat16 [3584, 512], P('rep'), may hold values from -1 to 1
- student_value: bfloat16 [3584, 512], P('rep'), may hold values from -0.09375 to 0.09375
- student_output: bfloat16 [3584, 2048], P('rep', 'shard'), may hold values from -0.125 to 0.125
- projection: bfloat16 [3584, 5120], P('rep', 'shard'), may hold values from -0.09375 to 0.09375
Outputs:
- query_grad: float32 [3584, 2048], P('rep', 'shard')
- output_grad: float32 [3584, 2048], P('rep', 'shard')
All inputs are finite; a program needn't handle non-finite values.
Results may differ from a plain program's by a relative error of at most 0.023.
Values may be sent and summed in bfloat16 or wider, within the bound.
A program may use at most 128 MiB of HBM per device.

v0:
```python
from functools import partial
import math
import jax
import jax.numpy as jnp
from jax import lax
from jax.sharding import PartitionSpec as P

HQ_S = 16
KV_S = 4
HD = 128
theta_base = 1000000.0
norm_epsilon = 1e-06


def rms_scale(states, gain):
    values = states.astype(jnp.float32)
    meansq = jnp.mean(values * values, axis=-1, keepdims=True)
    return (values * lax.rsqrt(meansq + norm_epsilon) * gain).astype(jnp.bfloat16)


def rotate(values, head_dim, turning):
    length = values.shape[0]
    halfway = head_dim // 2
    inverse = theta_base ** (-(jnp.arange(halfway, dtype=jnp.float32) * 2.0 / head_dim))
    angles = jnp.arange(length, dtype=jnp.float32)[:, None] * inverse[None, :]
    cosine = jnp.cos(angles)[:, None, :]
    sine = turning * jnp.sin(angles)[:, None, :]
    split = values.reshape(length, -1, head_dim)
    former = split[..., :halfway]
    latter = split[..., halfway:]
    turned = jnp.concatenate(
        [former * cosine - latter * sine, latter * cosine + former * sine], axis=-1
    )
    return turned.reshape(length, -1)


def attend(query_rot, keys, values, head_dim):
    length = query_rot.shape[0]
    kv_heads = keys.shape[1] // head_dim
    group_size = query_rot.shape[1] // head_dim // kv_heads
    queries = query_rot.astype(jnp.bfloat16).reshape(length, kv_heads, group_size, head_dim)
    key_heads = keys.reshape(length, kv_heads, head_dim)
    value_heads = values.reshape(length, kv_heads, head_dim)
    scores = jnp.einsum(
        "qkgd,skd->kgqs", queries, key_heads, preferred_element_type=jnp.float32
    ) * head_dim ** (-0.5)
    rows_index = jnp.arange(length)[:, None]
    column_index = jnp.arange(length)[None, :]
    scores = jnp.where(rows_index >= column_index, scores, -1e30)
    highest = jnp.max(scores, axis=-1, keepdims=True)
    weights = jnp.exp(scores - highest)
    probs = (weights / jnp.sum(weights, axis=-1, keepdims=True)).astype(jnp.bfloat16)
    mixed = jnp.einsum("kgqs,skd->qkgd", probs, value_heads, preferred_element_type=jnp.float32)
    return mixed.reshape(length, -1)


def teacher_side(states, gain, query_w, key_w, value_w, output_w):
    normed = rms_scale(states, gain)
    queries = rotate(jnp.dot(normed, query_w, preferred_element_type=jnp.float32), HD, 1.0)
    keys = rotate(jnp.dot(normed, key_w, preferred_element_type=jnp.float32), HD, 1.0).astype(
        jnp.bfloat16
    )
    values = jnp.dot(normed, value_w, preferred_element_type=jnp.float32).astype(jnp.bfloat16)
    mixed = attend(queries, keys, values, HD).astype(jnp.bfloat16)
    return jnp.dot(mixed, output_w.T, preferred_element_type=jnp.float32)


def student_side(states, gain, query_w, key_w, value_w, output_w):
    normed = rms_scale(states, gain)
    queries = rotate(jnp.dot(normed, query_w, preferred_element_type=jnp.float32), HD, 1.0)
    keys = rotate(jnp.dot(normed, key_w, preferred_element_type=jnp.float32), HD, 1.0).astype(
        jnp.bfloat16
    )
    values = jnp.dot(normed, value_w, preferred_element_type=jnp.float32).astype(jnp.bfloat16)
    mixed_full, pullback = jax.vjp(partial(attend, keys=keys, values=values, head_dim=HD), queries)
    mixed = mixed_full.astype(jnp.bfloat16)
    partial_out = jnp.dot(mixed, output_w.T, preferred_element_type=jnp.float32)
    return (normed, mixed, pullback, partial_out)


def local(
    teacher_states,
    student_states,
    teacher_gain,
    student_gain,
    teacher_query,
    teacher_key,
    teacher_value,
    teacher_output,
    student_query,
    student_key,
    student_value,
    student_output,
    projection,
):
    shard_index = lax.axis_index("shard")
    length = teacher_states.shape[0]
    local_heads = student_query.shape[1] // HD
    group_size = HQ_S // KV_S
    kv_count = max(local_heads // group_size, 1)
    kv_start = shard_index * local_heads // group_size * HD
    key_slice = lax.dynamic_slice_in_dim(student_key, kv_start, kv_count * HD, 1)
    value_slice = lax.dynamic_slice_in_dim(student_value, kv_start, kv_count * HD, 1)
    gathered = (
        lax.all_gather(teacher_query, "rep", axis=0, tiled=True),
        lax.all_gather(teacher_key, "rep", axis=0, tiled=True),
        lax.all_gather(teacher_value, "rep", axis=0, tiled=True),
        lax.all_gather(teacher_output, "rep", axis=0, tiled=True),
        lax.all_gather(student_query, "rep", axis=0, tiled=True),
        lax.all_gather(key_slice, "rep", axis=0, tiled=True),
        lax.all_gather(value_slice, "rep", axis=0, tiled=True),
        lax.all_gather(student_output, "rep", axis=0, tiled=True),
        lax.all_gather(projection, "rep", axis=0, tiled=True),
    )
    teacher_partial = teacher_side(
        teacher_states, teacher_gain, gathered[0], gathered[1], gathered[2], gathered[3]
    )
    student_weights_full = gathered[4:]
    query_full, key_full, value_full, output_full, column_map = student_weights_full
    normed_s, mixed_s, pullback, student_partial = student_side(
        student_states, student_gain, query_full, key_full, value_full, output_full
    )
    block_width = column_map.shape[1]
    attn_block = lax.psum_scatter(
        teacher_partial.astype(jnp.bfloat16), "shard", scatter_dimension=1, tiled=True
    ).astype(jnp.float32)
    attn_student = lax.psum(student_partial.astype(jnp.bfloat16), "shard").astype(jnp.float32)
    own_states = lax.dynamic_slice_in_dim(teacher_states, shard_index * block_width, block_width, 1)
    teacher_hidden = own_states.astype(jnp.float32) + attn_block
    student_hidden = (student_states.astype(jnp.float32) + attn_student).astype(jnp.bfloat16)
    scaling = 1.0 / math.sqrt(lax.axis_size("rep") * length)
    predicted = jnp.dot(student_hidden, column_map, preferred_element_type=jnp.float32)
    grad_pred = ((predicted - teacher_hidden) * scaling).astype(jnp.bfloat16)
    back_term = jnp.dot(grad_pred, column_map.T, preferred_element_type=jnp.float32)
    grad_hidden = lax.psum(back_term.astype(jnp.bfloat16), "shard")
    grad_mixed = jnp.dot(grad_hidden, output_full, preferred_element_type=jnp.float32)
    grad_rot = pullback(grad_mixed)[0]
    grad_query = rotate(grad_rot, HD, -1.0).astype(jnp.bfloat16)
    out_term = jnp.dot(grad_hidden.T, mixed_s, preferred_element_type=jnp.float32)
    query_term = jnp.dot(normed_s.T, grad_query, preferred_element_type=jnp.float32)
    query_grad, output_grad = (
        lax.psum_scatter(
            query_term.astype(jnp.bfloat16), "rep", scatter_dimension=0, tiled=True
        ).astype(jnp.float32),
        lax.psum_scatter(
            out_term.astype(jnp.bfloat16), "rep", scatter_dimension=0, tiled=True
        ).astype(jnp.float32),
    )
    return (query_grad, output_grad)


def solution(mesh):
    return jax.shard_map(
        local,
        mesh=mesh,
        in_specs=(
            P("rep", None),
            P("rep", None),
            P(),
            P(),
            P("rep", "shard"),
            P("rep", "shard"),
            P("rep", "shard"),
            P("rep", "shard"),
            P("rep", "shard"),
            P("rep", None),
            P("rep", None),
            P("rep", "shard"),
            P("rep", "shard"),
        ),
        out_specs=(P("rep", "shard"), P("rep", "shard")),
        check_vma=False,
    )
```

profile of v0, /device:TPU:0, one launch (start us, length us, event | category | flops | bytes accessed | tf_op | source)
XLA Modules:
  0.0 741.3 jit_solution(9428852129858372439)
XLA Ops:
  7.2 0.7 all-gather.8.cloned.1.call-update
  8.0 0.7 all-gather.10.cloned.1.call-update
  8.7 0.7 all-gather.16.cloned.1.call-update
  11.3 0.9 constant_dynamic-slice_fusion.1
  12.2 13.5 %all_gather.28 = bf16[3584,128]{1,0:T(8,128)(2,1)S(1)} all-gather(bf16[448,128]{1,0:T(8,128)(2,1)S(1)} %constant_dynamic-slice_fusion), channel_id=1, replica_groups=mesh['rep'=8,'shard'=4] {'rep'}, dimensions={0}, use_global_device_ids=true | all-gather | bytes 1032192 | tf_op jit(solution)/shard_map/all_gather | solution.py:110
  25.7 11.7 %all_gather.27 = bf16[3584,128]{1,0:T(8,128)(2,1)S(1)} all-gather(bf16[448,128]{1,0:T(8,128)(2,1)S(1)} %constant_dynamic-slice_fusion.1), channel_id=1, replica_groups=mesh['rep'=8,'shard'=4] {'rep'}, dimensions={0}, use_global_device_ids=true | all-gather | bytes 1032192 | tf_op jit(solution)/shard_map/all_gather | solution.py:111
  38.1 1.1 convolution_bitcast_fusion
  39.7 1.4 broadcast_multiply_fusion
  41.1 0.9 fusion.42
  42.1 5.9 all-gather.8.cloned.1.call-done
  47.9 4.6 fusion.75
  52.5 1.4 reshape.234
  54.6 0.7 fusion.25
  55.8 0.9 convolution_convert_fusion.6
  56.7 27.8 %all-gather.10.cloned.1.call-done = bf16[3584,512]{1,0:T(8,128)(2,1)} async-done(((bf16[448,512]{1,0:T(8,128)(2,1)}), bf16[3584,512]{1,0:T(8,128)(2,1)}) %all-gather.10.cloned.1.call-update) | async-done | bytes 3670032 | tf_op jit(solution)/shard_map/all_gather | solution.py:112
  84.6 5.2 convolution_convert_fusion.4
  89.8 0.7 all-gather.12.cloned.1.call-update
  91.3 3.1 fusion.1
  94.9 21.6 %all-gather.16.cloned.1.call-done = bf16[5120,256]{1,0:T(8,128)(2,1)} async-done(((bf16[640,256]{1,0:T(8,128)(2,1)}), bf16[5120,256]{1,0:T(8,128)(2,1)}) %all-gather.16.cloned.1.call-update) | async-done | bytes 2621456 | tf_op jit(solution)/shard_map/all_gather | solution.py:106
  116.5 4.7 fusion.71
  121.2 0.8 fusion.81
  121.9 1.1 copy.54
  123.0 1.8 copy.55
  124.9 1.9 subtract_convert_fusion.3
  126.8 21.5 %all-gather.14.cloned.1.call-done = bf16[5120,256]{1,0:T(8,128)(2,1)} async-done(((bf16[640,256]{1,0:T(8,128)(2,1)}), bf16[5120,256]{1,0:T(8,128)(2,1)}) %all-gather.14.cloned.1.call-update) | async-done | bytes 2621456 | tf_op jit(solution)/shard_map/all_gather | solution.py:107
  148.2 5.4 convolution_convert_fusion.7
  153.6 48.5 %all-gather.18.cloned.1.call-done = bf16[5120,768]{1,0:T(8,128)(2,1)} async-done(((bf16[640,768]{1,0:T(8,128)(2,1)}), bf16[5120,768]{1,0:T(8,128)(2,1)}) %all-gather.18.cloned.1.call-update) | async-done | bytes 7864336 | tf_op jit(solution)/shard_map/all_gather | solution.py:105
  202.0 8.0 %fusion.69 = f32[384,768]{0,1:T(8,128)S(1)} fusion(bf16[5120,768]{1,0:T(8,128)(2,1)} %all-gather.18.cloned.1.call-done, bf16[384,5120]{1,0:T(8,128)(2,1)} %param.13, f32[5120]{0:T(1024)S(1)} %copy-done.10, f32[384]{0:T(512)S(1)} %copy-done.9), kind=kOutput, calls=%fused_computation.110 | convolution fusion | flops 3027763200 | bytes 12998144 | tf_op jit(solution)/shard_map/dot_general | solution.py:59
  210.3 4.2 fusion.82
  214.5 2.6 fusion.30
  217.1 38.7 %all-gather.20.cloned.1.call-done = bf16[5120,768]{1,0:T(8,128)(2,1)} async-done(((bf16[640,768]{1,0:T(8,128)(2,1)}), bf16[5120,768]{1,0:T(8,128)(2,1)}) %all-gather.20.cloned.1.call-update) | async-done | bytes 7864336 | tf_op jit(solution)/shard_map/all_gather | solution.py:108
  255.9 8.4 %convolution_convert_fusion = bf16[384,5120]{1,0:T(8,128)(2,1)} fusion(bf16[384,768]{0,1:T(8,128)(2,1)S(1)} %bitcast.146, bf16[5120,768]{1,0:T(8,128)(2,1)} %all-gather.20.cloned.1.call-done), kind=kOutput, calls=%fused_computation.9 | convolution fusion | flops 3021864960 | bytes 12386304 | tf_op jit(solution)/shard_map/dot_general | solution.py:65
  264.5 102.1 %all-reduce.3.cloned.1.call-done = bf16[384,3584]{1,0:T(8,128)(2,1)} async-done(((bf16[384,3584]{1,0:T(8,128)(2,1)}), bf16[384,3584]{1,0:T(8,128)(2,1)}) %all-reduce.3.cloned.1.call-update) | async-done | bytes 2752528 | tf_op jit(solution)/shard_map/psum | solution.py:127
  366.6 58.5 %all-gather.12.cloned.1.call-done = bf16[3584,1280]{1,0:T(8,128)(2,1)} async-done(((bf16[448,1280]{1,0:T(8,128)(2,1)}), bf16[3584,1280]{1,0:T(8,128)(2,1)}) %all-gather.12.cloned.1.call-update) | async-done | bytes 9175056 | tf_op jit(solution)/shard_map/all_gather | solution.py:113
  425.1 75.0 %reduce-scatter.4.cloned.1.call-done = bf16[384,1280]{1,0:T(8,128)(2,1)} async-done(((bf16[384,5120]{1,0:T(8,128)(2,1)}), bf16[384,1280]{1,0:T(8,128)(2,1)}) %reduce-scatter.4.cloned.1.call-update) | async-done | bytes 983056 | tf_op jit(solution)/shard_map/reduce_scatter | solution.py:124
  500.1 17.8 %convolution_convert_fusion.3 = bf16[384,3584]{1,0:T(8,128)(2,1)} fusion(bf16[3584,1280]{1,0:T(8,128)(2,1)} %all-gather.12.cloned.1.call-done, bf16[384,3584]{1,0:T(8,128)(2,1)} %param.14, bf16[384,3584]{1,0:T(8,128)(2,1)} %all-reduce.3.cloned.1.call-done, bf16[384,1280]{1,0:T(8,128)(2,1)} %reduce-scatter.4.cloned.1.call-done, ...), kind=kOutput, calls=%fused_computation.12 | convolution fusion | flops 7056261120 | bytes 28573700 | tf_op jit(solution)/shard_map/dot_general | solution.py:134
  518.0 108.9 %all-reduce.5.cloned.1.call-done = bf16[384,3584]{1,0:T(8,128)(2,1)} async-done(((bf16[384,3584]{1,0:T(8,128)(2,1)}), bf16[384,3584]{1,0:T(8,128)(2,1)}) %all-reduce.5.cloned.1.call-update) | async-done | bytes 2752528 | tf_op jit(solution)/shard_map/psum | solution.py:135
  626.8 5.7 convolution_convert_fusion.1
  632.8 5.0 fusion.83
  637.9 0.8 fusion.17
  638.7 1.3 convert_reduce_fusion
  640.1 1.6 fusion.34
  642.3 0.9 copy.40
  643.8 5.1 convolution_convert_fusion.2
  649.0 31.3 %reduce-scatter.8.cloned.1.call-done = bf16[448,512]{1,0:T(8,128)(2,1)} async-done(((bf16[3584,512]{1,0:T(8,128)(2,1)}), bf16[448,512]{1,0:T(8,128)(2,1)}) %reduce-scatter.8.cloned.1.call-update) | async-done | bytes 458768 | tf_op jit(solution)/shard_map/reduce_scatter | solution.py:145
  680.3 2.1 convert_element_type.152
  682.3 49.9 %reduce-scatter.6.cloned.1.call-done = bf16[448,512]{1,0:T(8,128)(2,1)} async-done(((bf16[3584,512]{1,0:T(8,128)(2,1)}), bf16[448,512]{1,0:T(8,128)(2,1)}) %reduce-scatter.6.cloned.1.call-update) | async-done | bytes 458768 | tf_op jit(solution)/shard_map/reduce_scatter | solution.py:142
  732.2 2.1 convert_element_type.150
  (73 shorter events, 7.7 us)
Async XLA Ops:
  7.2 4.1 copy-start
  7.2 40.8 %all-gather.8.cloned.1.call-start = ((), (), s32[]{:S(2)}) async-start(), calls=%async_computation.3 | async-start | bytes 4128768 | tf_op jit(solution)/shard_map/all_gather | solution.py:109
  7.9 76.7 %all-gather.10.cloned.1.call-start = ((), (), s32[]{:S(2)}) async-start(), calls=%async_computation.4 | async-start | bytes 4128768 | tf_op jit(solution)/shard_map/all_gather | solution.py:112
  8.7 28.8 %copy-start.2 = (bf16[384,3584]{1,0:T(8,128)(2,1)S(1)}, bf16[384,3584]{1,0:T(8,128)(2,1)}, u32[]{:S(2)}) copy-start(bf16[384,3584]{1,0:T(8,128)(2,1)} %param.14) | copy-start | bytes 8257540
  8.7 107.8 %all-gather.16.cloned.1.call-start = ((), (), s32[]{:S(2)}) async-start(), calls=%async_computation.8 | async-start | bytes 2949120 | tf_op jit(solution)/shard_map/all_gather | solution.py:106
  9.4 138.8 %all-gather.14.cloned.1.call-start = ((), (), s32[]{:S(2)}) async-start(), calls=%async_computation.7 | async-start | bytes 2949120 | tf_op jit(solution)/shard_map/all_gather | solution.py:107
  10.0 192.1 %all-gather.18.cloned.1.call-start = ((), (), s32[]{:S(2)}) async-start(), calls=%async_computation.9 | async-start | bytes 8847360 | tf_op jit(solution)/shard_map/all_gather | solution.py:105
  10.6 245.3 %all-gather.20.cloned.1.call-start = ((), (), s32[]{:S(2)}) async-start(), calls=%async_computation.10 | async-start | bytes 8847360 | tf_op jit(solution)/shard_map/all_gather | solution.py:108
  11.2 26.9 %copy-start.11 = (f32[3584]{0:T(1024)S(1)}, f32[3584]{0:T(1024)}, u32[]{:S(2)}) copy-start(f32[3584]{0:T(1024)} %param.16) | copy-start | bytes 43012
  11.2 355.4 %all-reduce.3.cloned.1.call-start = ((), (), s32[]{:S(2)}) async-start(), calls=%async_computation.5 | async-start | bytes 5505024 | tf_op jit(solution)/shard_map/psum | solution.py:127
  38.1 9.9 %copy-start.7 = (f32[384]{0:T(512)}, f32[384]{0:T(512)S(1)}, u32[]{:S(2)}) copy-start(f32[384]{0:T(512)S(1)} %add_rsqrt_fusion.1) | copy-start | bytes 4612
  39.7 14.9 %copy-start.5 = (bf16[384,64]{0,1:T(8,128)(2,1)}, bf16[384,64]{0,1:T(8,128)(2,1)S(1)}, u32[]{:S(2)}) copy-start(bf16[384,64]{0,1:T(8,128)(2,1)S(1)} %get-tuple-element.18) | copy-start | bytes 147460
  42.1 13.8 %copy-start.15 = (bf16[384,128,1]{1,0,2:T(8,128)(2,1)}, bf16[384,128,1]{1,0,2:T(8,128)(2,1)S(1)}, u32[]{:S(2)}) copy-start(bf16[384,128,1]{1,0,2:T(8,128)(2,1)S(1)} %fusion.42) | copy-start | bytes 294916
  56.7 33.0 %copy-start.13 = (bf16[128,4,384]{2,0,1:T(8,128)(2,1)}, bf16[128,4,384]{2,0,1:T(8,128)(2,1)S(1)}, u32[]{:S(2)}) copy-start(bf16[128,4,384]{2,0,1:T(8,128)(2,1)S(1)} %convolution_convert_fusion.6) | copy-start | bytes 1179652
  89.8 335.3 %all-gather.12.cloned.1.call-start = ((), (), s32[]{:S(2)}) async-start(), calls=%async_computation.6 | async-start | bytes 10321920 | tf_op jit(solution)/shard_map/all_gather | solution.py:113
  90.5 409.5 %reduce-scatter.4.cloned.1.call-start = ((), (), s32[]{:S(2)}) async-start(), calls=%async_computation.11 | async-start | bytes 4915200 | tf_op jit(solution)/shard_map/reduce_scatter | solution.py:124
  126.7 75.3 %copy-start.9 = (f32[384]{0:T(512)S(1)}, f32[384]{0:T(512)}, u32[]{:S(2)}) copy-start(f32[384]{0:T(512)} %add_rsqrt_fusion) | copy-start | bytes 4612
  126.8 75.3 %copy-start.10 = (f32[5120]{0:T(1024)S(1)}, f32[5120]{0:T(1024)}, u32[]{:S(2)}) copy-start(f32[5120]{0:T(1024)} %param.15) | copy-start | bytes 61444
  264.2 362.6 %all-reduce.5.cloned.1.call-start = ((), (), s32[]{:S(2)}) async-start(), calls=%async_computation.12 | async-start | bytes 5505024 | tf_op jit(solution)/shard_map/psum | solution.py:135
  517.9 108.9 %copy-start.14 = (bf16[128,4,384]{2,0,1:T(8,128)(2,1)S(1)}, bf16[128,4,384]{2,0,1:T(8,128)(2,1)}, u32[]{:S(2)}) copy-start(bf16[128,4,384]{2,0,1:T(8,128)(2,1)} %copy-done.13) | copy-start | bytes 1179652
  517.9 162.4 %reduce-scatter.8.cloned.1.call-start = ((), (), s32[]{:S(2)}) async-start(), calls=%async_computation.14 | async-start | bytes 4128768 | tf_op jit(solution)/shard_map/reduce_scatter | solution.py:145
  632.6 99.6 %reduce-scatter.6.cloned.1.call-start = ((), (), s32[]{:S(2)}) async-start(), calls=%async_computation.13 | async-start | bytes 4128768 | tf_op jit(solution)/shard_map/reduce_scatter | solution.py:142
  632.8 5.0 copy-start.16
  638.7 1.3 copy-start.6
  640.1 1.6 copy-start.4
  641.6 2.2 copy-start.3
  641.6 2.2 copy-start.8
  641.7 2.2 copy-start.12
  648.9 85.3 %copy-start.1 = (bf16[448,512]{1,0:T(8,128)(2,1)S(1)}, bf16[448,512]{1,0:T(8,128)(2,1)}, u32[]{:S(2)}) copy-start(bf16[448,512]{1,0:T(8,128)(2,1)} %param.22) | copy-start | bytes 1376260
Sparse Core Ops, SparseCore 0:
  9.9 38.0 all-gather.7
  49.8 34.6 all-gather.9
  86.5 29.9 all-gather.15
  118.2 29.9 all-gather.13
  150.0 52.0 all-gather.17
  203.8 52.0 all-gather.19
  258.2 108.3 all-reduce.2
  368.5 56.5 all-gather.11
  427.4 72.6 reduce-scatter.3
  518.0 108.7 all-reduce.4
  632.7 47.5 reduce-scatter.7
  683.6 48.5 reduce-scatter.5
where the time goes:
time: 750 us; the launch traced here: 741 us
  waiting for transfers between devices  594 us (79%)
  matrix products  82.6 us (11%)
  blocking collectives  25.2 us (3%)
  other arithmetic  15.1 us (2%)
  between operations  14.8 us (2%)
  local copies, waits for them, and re-layouts  8.35 us (1%)
    psum x1, waiting for transfers between devices, local(): grad_hidden = lax.psum(back_term.astype(jnp.bfloat16), 'shard')  109 us
    psum x1, waiting for transfers between devices, local(): lax.psum(student_partial.astype(jnp.bfloat16), 'shard').astype(jnp.float32)  102 us
    reduce_scatter x1, waiting for transfers between devices, local(): lax.psum_scatter(teacher_partial.astype(jnp.bfloat16), 'shard', scatter_d...  75 us
    all_gather x1, waiting for transfers between devices, local(): lax.all_gather(projection, 'rep', axis=0, tiled=True)  58.5 us
    reduce_scatter x1, waiting for transfers between devices, local(): lax.psum_scatter(query_term.astype(jnp.bfloat16), 'rep', scatter_dimensio...  49.9 us
    all_gather x1, waiting for transfers between devices, local(): lax.all_gather(teacher_query, 'rep', axis=0, tiled=True)  48.5 us
    all_gather x1, waiting for transfers between devices, local(): lax.all_gather(teacher_output, 'rep', axis=0, tiled=True)  38.7 us
    reduce_scatter x1, waiting for transfers between devices, local(): lax.psum_scatter(out_term.astype(jnp.bfloat16), 'rep', scatter_dimension=...  31.3 us
  transfers between devices with their start and end apart: 12, of which 12 were waited for; matrix products, arithmetic and copies ran while one was open for 11% of the time, Pallas kernels for 0%

commit v1 on v0

--- a/solution.py
+++ b/solution.py
@@ -10,6 +10,12 @@
 HD = 128
 theta_base = 1000000.0
 norm_epsilon = 1e-06
+
+
+def add_all(shard, mesh_axis):
+    pieces = lax.all_gather(shard, mesh_axis, axis=0, tiled=False)
+    total = pieces.sum(axis=0)
+    return total
 
 
 def rms_scale(states, gain):
@@ -124,7 +130,7 @@
     attn_block = lax.psum_scatter(
         teacher_partial.astype(jnp.bfloat16), "shard", scatter_dimension=1, tiled=True
     ).astype(jnp.float32)
-    attn_student = lax.psum(student_partial.astype(jnp.bfloat16), "shard").astype(jnp.float32)
+    attn_student = add_all(student_partial.astype(jnp.bfloat16), "shard").astype(jnp.float32)
     own_states = lax.dynamic_slice_in_dim(teacher_states, shard_index * block_width, block_width, 1)
     teacher_hidden = own_states.astype(jnp.float32) + attn_block
     student_hidden = (student_states.astype(jnp.float32) + attn_student).astype(jnp.bfloat16)

time: 750 us -> 833 us (1.11)
  waiting for transfers between devices: 594 us -> 667 us
    all_gather x0 -> x1, waiting for transfers between devices: none -> 185 us  [add_all(): pieces = lax.all_gather(shard, mesh_axis, axis=0, tiled=False)]
    psum x1 -> x0, waiting for transfers between devices: 102 us -> none  [local(): lax.psum(student_partial.astype(jnp.bfloat16), 'shard').astype(jnp.float32)]
    all_gather x1, waiting for transfers between devices: 58.5 us -> 49.6 us  [local(): lax.all_gather(projection, 'rep', axis=0, tiled=True)]
where the time goes in v1:
time: 833 us; the launch traced here: 824 us
  waiting for transfers between devices  667 us (80%)
  matrix products  84.1 us (10%)
  blocking collectives  25.2 us (3%)
  other arithmetic  23.4 us (3%)
  between operations  14.8 us (2%)
  local copies, waits for them, and re-layouts  8.64 us (1%)
    all_gather x1, waiting for transfers between devices, add_all(): pieces = lax.all_gather(shard, mesh_axis, axis=0, tiled=False)  185 us
    psum x1, waiting for transfers between devices, local(): grad_hidden = lax.psum(back_term.astype(jnp.bfloat16), 'shard')  109 us
    reduce_scatter x1, waiting for transfers between devices, local(): lax.psum_scatter(teacher_partial.astype(jnp.bfloat16), 'shard', scatter_d...  75 us
    reduce_scatter x1, waiting for transfers between devices, local(): lax.psum_scatter(query_term.astype(jnp.bfloat16), 'rep', scatter_dimensio...  49.9 us
    all_gather x1, waiting for transfers between devices, local(): lax.all_gather(projection, 'rep', axis=0, tiled=True)  49.6 us
    all_gather x1, waiting for transfers between devices, local(): lax.all_gather(teacher_query, 'rep', axis=0, tiled=True)  48.4 us
    all_gather x1, waiting for transfers between devices, local(): lax.all_gather(teacher_output, 'rep', axis=0, tiled=True)  36.9 us
    reduce_scatter x1, waiting for transfers between devices, local(): lax.psum_scatter(out_term.astype(jnp.bfloat16), 'rep', scatter_dimension=...  31.3 us
  transfers between devices with their start and end apart: 12, of which 12 were waited for; matrix products, arithmetic and copies ran while one was open for 11% of the time, Pallas kernels for 0%

profile of v1, /device:TPU:0, one launch (start us, length us, event | category | flops | bytes accessed | tf_op | source)
XLA Modules:
  0.0 824.0 jit_solution(14518701641345884205)
XLA Ops:
  11.3 0.9 constant_dynamic-slice_fusion.1
  12.2 13.5 %all_gather.34 = bf16[3584,128]{1,0:T(8,128)(2,1)S(1)} all-gather(bf16[448,128]{1,0:T(8,128)(2,1)S(1)} %constant_dynamic-slice_fusion), channel_id=1, replica_groups=mesh['rep'=8,'shard'=4] {'rep'}, dimensions={0}, use_global_device_ids=true | all-gather | bytes 1032192 | tf_op jit(solution)/shard_map/all_gather | solution.py:116
  25.7 11.7 %all_gather.33 = bf16[3584,128]{1,0:T(8,128)(2,1)S(1)} all-gather(bf16[448,128]{1,0:T(8,128)(2,1)S(1)} %constant_dynamic-slice_fusion.1), channel_id=1, replica_groups=mesh['rep'=8,'shard'=4] {'rep'}, dimensions={0}, use_global_device_ids=true | all-gather | bytes 1032192 | tf_op jit(solution)/shard_map/all_gather | solution.py:117
  38.1 1.1 convolution_bitcast_fusion
  39.7 1.4 broadcast_multiply_fusion
  41.1 0.9 fusion.42
  42.1 5.8 all-gather.10.cloned.1.call-done
  47.9 4.5 fusion.75
  52.5 1.4 reshape.234
  54.6 0.7 fusion.25
  55.8 0.9 convolution_convert_fusion.6
  56.7 27.9 %all-gather.12.cloned.1.call-done = bf16[3584,512]{1,0:T(8,128)(2,1)} async-done(((bf16[448,512]{1,0:T(8,128)(2,1)}), bf16[3584,512]{1,0:T(8,128)(2,1)}) %all-gather.12.cloned.1.call-update) | async-done | bytes 3670032 | tf_op jit(solution)/shard_map/all_gather | solution.py:118
  84.6 5.3 convolution_convert_fusion.4
  91.1 0.7 copy.34
  91.9 0.7 copy.35
  92.6 3.1 fusion.1
  95.8 20.7 %all-gather.18.cloned.1.call-done = bf16[5120,256]{1,0:T(8,128)(2,1)} async-done(((bf16[640,256]{1,0:T(8,128)(2,1)}), bf16[5120,256]{1,0:T(8,128)(2,1)}) %all-gather.18.cloned.1.call-update) | async-done | bytes 2621456 | tf_op jit(solution)/shard_map/all_gather | solution.py:112
  116.5 4.7 fusion.71
  121.2 0.7 fusion.81
  121.9 1.1 copy.54
  123.0 0.9 copy.55
  123.9 1.8 subtract_convert_fusion.3
  125.7 22.6 %all-gather.16.cloned.1.call-done = bf16[5120,256]{1,0:T(8,128)(2,1)} async-done(((bf16[640,256]{1,0:T(8,128)(2,1)}), bf16[5120,256]{1,0:T(8,128)(2,1)}) %all-gather.16.cloned.1.call-update) | async-done | bytes 2621456 | tf_op jit(solution)/shard_map/all_gather | solution.py:113
  148.2 5.4 convolution_convert_fusion.7
  153.6 48.4 %all-gather.20.cloned.1.call-done = bf16[5120,768]{1,0:T(8,128)(2,1)} async-done(((bf16[640,768]{1,0:T(8,128)(2,1)}), bf16[5120,768]{1,0:T(8,128)(2,1)}) %all-gather.20.cloned.1.call-update) | async-done | bytes 7864336 | tf_op jit(solution)/shard_map/all_gather | solution.py:111
  202.0 8.0 fusion.69
  210.2 0.9 pad_maximum_fusion
  211.1 4.5 fusion.82
  215.6 3.3 fusion.30
  218.9 36.9 %all-gather.22.cloned.1.call-done = bf16[5120,768]{1,0:T(8,128)(2,1)} async-done(((bf16[640,768]{1,0:T(8,128)(2,1)}), bf16[5120,768]{1,0:T(8,128)(2,1)}) %all-gather.22.cloned.1.call-update) | async-done | bytes 7864336 | tf_op jit(solution)/shard_map/all_gather | solution.py:114
  255.9 8.7 %convolution_convert_fusion = bf16[384,5120]{1,0:T(8,128)(2,1)} fusion(bf16[384,768]{0,1:T(8,128)(2,1)} %bitcast.148, bf16[5120,768]{1,0:T(8,128)(2,1)} %all-gather.22.cloned.1.call-done), kind=kOutput, calls=%fused_computation.9 | convolution fusion | flops 3021864960 | bytes 12386304 | tf_op jit(solution)/shard_map/dot_general | solution.py:71
  264.8 185.1 %all-gather.24.cloned.1.call-done = bf16[1536,3584]{1,0:T(8,128)(2,1)} async-done(((bf16[384,3584]{1,0:T(8,128)(2,1)}), bf16[1536,3584]{1,0:T(8,128)(2,1)}) %all-gather.24.cloned.1.call-update) | async-done | bytes 11010064 | tf_op jit(solution)/shard_map/all_gather | solution.py:16
  449.9 8.1 reduce_sum.85
  458.0 49.6 %all-gather.14.cloned.1.call-done = bf16[3584,1280]{1,0:T(8,128)(2,1)} async-done(((bf16[448,1280]{1,0:T(8,128)(2,1)}), bf16[3584,1280]{1,0:T(8,128)(2,1)}) %all-gather.14.cloned.1.call-update) | async-done | bytes 9175056 | tf_op jit(solution)/shard_map/all_gather | solution.py:119
  507.6 75.0 %reduce-scatter.4.cloned.1.call-done = bf16[384,1280]{1,0:T(8,128)(2,1)} async-done(((bf16[384,5120]{1,0:T(8,128)(2,1)}), bf16[384,1280]{1,0:T(8,128)(2,1)}) %reduce-scatter.4.cloned.1.call-update) | async-done | bytes 983056 | tf_op jit(solution)/shard_map/reduce_scatter | solution.py:130
  582.6 18.0 %convolution_convert_fusion.3 = bf16[384,3584]{1,0:T(8,128)(2,1)} fusion(bf16[3584,1280]{1,0:T(8,128)(2,1)} %all-gather.14.cloned.1.call-done, bf16[384,3584]{1,0:T(8,128)(2,1)} %param.14, bf16[384,3584]{1,0:T(8,128)(2,1)} %reduce_sum.85, bf16[384,1280]{1,0:T(8,128)(2,1)} %reduce-scatter.4.cloned.1.call-done, bf16[384,5120]{1,0:T(8,128)(2,1)} %param.13, ...), kind=kOutput, calls=%fused_computation.12 | convolution fusion | flops 7056261120 | bytes 28573700 | tf_op jit(solution)/shard_map/dot_general | solution.py:140
  600.6 108.9 %all-reduce.2.cloned.1.call-done = bf16[384,3584]{1,0:T(8,128)(2,1)} async-done(((bf16[384,3584]{1,0:T(8,128)(2,1)}), bf16[384,3584]{1,0:T(8,128)(2,1)}) %all-reduce.2.cloned.1.call-update) | async-done | bytes 2752528 | tf_op jit(solution)/shard_map/psum | solution.py:141
  709.5 5.7 convolution_convert_fusion.1
  715.5 5.0 fusion.83
  720.5 0.8 fusion.17
  721.4 1.3 convert_reduce_fusion
  722.7 1.6 fusion.34
  725.0 0.9 copy.40
  726.5 5.1 convolution_convert_fusion.2
  731.6 31.3 %reduce-scatter.8.cloned.1.call-done = bf16[448,512]{1,0:T(8,128)(2,1)} async-done(((bf16[3584,512]{1,0:T(8,128)(2,1)}), bf16[448,512]{1,0:T(8,128)(2,1)}) %reduce-scatter.8.cloned.1.call-update) | async-done | bytes 458768 | tf_op jit(solution)/shard_map/reduce_scatter | solution.py:151
  763.0 2.1 convert_element_type.154
  765.0 49.9 %reduce-scatter.6.cloned.1.call-done = bf16[448,512]{1,0:T(8,128)(2,1)} async-done(((bf16[3584,512]{1,0:T(8,128)(2,1)}), bf16[448,512]{1,0:T(8,128)(2,1)}) %reduce-scatter.6.cloned.1.call-update) | async-done | bytes 458768 | tf_op jit(solution)/shard_map/reduce_scatter | solution.py:148
  814.9 2.1 convert_element_type.152
  (84 shorter events, 9.6 us)
Async XLA Ops:
  7.2 4.1 copy-start
  7.2 40.8 %all-gather.10.cloned.1.call-start = ((), (), s32[]{:S(2)}) async-start(), calls=%async_computation.3 | async-start | bytes 4128768 | tf_op jit(solution)/shard_map/all_gather | solution.py:115
  7.9 76.7 %all-gather.12.cloned.1.call-start = ((), (), s32[]{:S(2)}) async-start(), calls=%async_computation.4 | async-start | bytes 4128768 | tf_op jit(solution)/shard_map/all_gather | solution.py:118
  8.7 28.8 %copy-start.2 = (bf16[384,3584]{1,0:T(8,128)(2,1)S(1)}, bf16[384,3584]{1,0:T(8,128)(2,1)}, u32[]{:S(2)}) copy-start(bf16[384,3584]{1,0:T(8,128)(2,1)} %param.14) | copy-start | bytes 8257540
  8.7 107.8 %all-gather.18.cloned.1.call-start = ((), (), s32[]{:S(2)}) async-start(), calls=%async_computation.7 | async-start | bytes 2949120 | tf_op jit(solution)/shard_map/all_gather | solution.py:112
  9.4 138.8 %all-gather.16.cloned.1.call-start = ((), (), s32[]{:S(2)}) async-start(), calls=%async_computation.6 | async-start | bytes 2949120 | tf_op jit(solution)/shard_map/all_gather | solution.py:113
  10.0 192.1 %all-gather.20.cloned.1.call-start = ((), (), s32[]{:S(2)}) async-start(), calls=%async_computation.8 | async-start | bytes 8847360 | tf_op jit(solution)/shard_map/all_gather | solution.py:111
  10.6 245.3 %all-gather.22.cloned.1.call-start = ((), (), s32[]{:S(2)}) async-start(), calls=%async_computation.9 | async-start | bytes 8847360 | tf_op jit(solution)/shard_map/all_gather | solution.py:114
  11.2 26.9 %copy-start.15 = (f32[3584]{0:T(1024)S(1)}, f32[3584]{0:T(1024)}, u32[]{:S(2)}) copy-start(f32[3584]{0:T(1024)} %param.16) | copy-start | bytes 43012
  11.2 438.8 %all-gather.24.cloned.1.call-start = ((), (), s32[]{:S(2)}) async-start(), calls=%async_computation.14 | async-start | bytes 13762560 | tf_op jit(solution)/shard_map/all_gather | solution.py:16
  38.1 9.9 %copy-start.9 = (f32[384]{0:T(512)}, f32[384]{0:T(512)S(1)}, u32[]{:S(2)}) copy-start(f32[384]{0:T(512)S(1)} %add_rsqrt_fusion.1) | copy-start | bytes 4612
  39.7 14.9 %copy-start.7 = (bf16[384,64]{0,1:T(8,128)(2,1)}, bf16[384,64]{0,1:T(8,128)(2,1)S(1)}, u32[]{:S(2)}) copy-start(bf16[384,64]{0,1:T(8,128)(2,1)S(1)} %get-tuple-element.18) | copy-start | bytes 147460
  42.1 13.7 %copy-start.20 = (bf16[384,128,1]{1,0,2:T(8,128)(2,1)}, bf16[384,128,1]{1,0,2:T(8,128)(2,1)S(1)}, u32[]{:S(2)}) copy-start(bf16[384,128,1]{1,0,2:T(8,128)(2,1)S(1)} %fusion.42) | copy-start | bytes 294916
  56.7 33.1 %copy-start.17 = (bf16[128,4,384]{2,0,1:T(8,128)(2,1)}, bf16[128,4,384]{2,0,1:T(8,128)(2,1)S(1)}, u32[]{:S(2)}) copy-start(bf16[128,4,384]{2,0,1:T(8,128)(2,1)S(1)} %convolution_convert_fusion.6) | copy-start | bytes 1179652
  89.9 26.6 %copy-start.13 = (f32[5120]{0:T(1024)S(1)}, f32[5120]{0:T(1024)}, u32[]{:S(2)}) copy-start(f32[5120]{0:T(1024)} %param.15) | copy-start | bytes 61444
  89.9 417.8 %all-gather.14.cloned.1.call-start = ((), (), s32[]{:S(2)}) async-start(), calls=%async_computation.5 | async-start | bytes 10321920 | tf_op jit(solution)/shard_map/all_gather | solution.py:119
  90.6 492.0 %reduce-scatter.4.cloned.1.call-start = ((), (), s32[]{:S(2)}) async-start(), calls=%async_computation.10 | async-start | bytes 4915200 | tf_op jit(solution)/shard_map/reduce_scatter | solution.py:130
  95.8 25.4 %copy-start.11 = (f32[384]{0:T(512)}, f32[384]{0:T(512)S(1)}, u32[]{:S(2)}) copy-start(f32[384]{0:T(512)S(1)} %add_rsqrt_fusion) | copy-start | bytes 4612
  125.7 76.4 %copy-start.12 = (f32[384]{0:T(512)S(1)}, f32[384]{0:T(512)}, u32[]{:S(2)}) copy-start(f32[384]{0:T(512)} %copy-done.11) | copy-start | bytes 4612
  125.7 76.4 %copy-start.14 = (f32[5120]{0:T(1024)S(1)}, f32[5120]{0:T(1024)}, u32[]{:S(2)}) copy-start(f32[5120]{0:T(1024)} %param.15) | copy-start | bytes 61444
  153.6 56.5 %copy-start.5 = (f32[384,64]{0,1:T(8,128)S(1)}, f32[384,64]{0,1:T(8,128)}, u32[]{:S(2)}) copy-start(f32[384,64]{0,1:T(8,128)} %copy.34) | copy-start | bytes 294916
  153.6 56.5 %copy-start.6 = (f32[384,64]{0,1:T(8,128)S(1)}, f32[384,64]{0,1:T(8,128)}, u32[]{:S(2)}) copy-start(f32[384,64]{0,1:T(8,128)} %copy.35) | copy-start | bytes 294916
  211.1 4.5 copy-start.19
  264.6 444.9 %all-reduce.2.cloned.1.call-start = ((), (), s32[]{:S(2)}) async-start(), calls=%async_computation.11 | async-start | bytes 5505024 | tf_op jit(solution)/shard_map/psum | solution.py:141
  600.6 109.0 %copy-start.18 = (bf16[128,4,384]{2,0,1:T(8,128)(2,1)S(1)}, bf16[128,4,384]{2,0,1:T(8,128)(2,1)}, u32[]{:S(2)}) copy-start(bf16[128,4,384]{2,0,1:T(8,128)(2,1)} %copy-done.17) | copy-start | bytes 1179652
  600.6 162.4 %reduce-scatter.8.cloned.1.call-start = ((), (), s32[]{:S(2)}) async-start(), calls=%async_computation.13 | async-start | bytes 4128768 | tf_op jit(solution)/shard_map/reduce_scatter | solution.py:151
  715.2 99.6 %reduce-scatter.6.cloned.1.call-start = ((), (), s32[]{:S(2)}) async-start(), calls=%async_computation.12 | async-start | bytes 4128768 | tf_op jit(solution)/shard_map/reduce_scatter | solution.py:148
  715.5 5.0 copy-start.21
  721.4 1.3 copy-start.8
  722.7 1.6 copy-start.4
  724.3 2.2 copy-start.3
  724.3 2.2 copy-start.10
  724.3 2.2 copy-start.16
  731.6 85.3 %copy-start.1 = (bf16[448,512]{1,0:T(8,128)(2,1)S(1)}, bf16[448,512]{1,0:T(8,128)(2,1)}, u32[]{:S(2)}) copy-start(bf16[448,512]{1,0:T(8,128)(2,1)} %param.22) | copy-start | bytes 1376260
Sparse Core Ops, SparseCore 0:
  9.9 38.0 all-gather.9
  49.8 34.7 all-gather.11
  86.5 29.9 all-gather.17
  118.2 29.9 all-gather.15
  150.0 52.0 all-gather.19
  203.8 52.0 all-gather.21
  257.4 192.4 all-gather.23
  451.8 55.7 all-gather.13
  509.9 72.6 reduce-scatter.3
  600.7 108.7 all-reduce.1
  715.3 47.5 reduce-scatter.7
  766.3 48.5 reduce-scatter.5
